TPU v7x, 32 devices: a whole 2x2x4 slice. The times are simulated.
32 devices in a mesh: dp: 8 (over z, x), expert: 4 (over y, core).
Axes of the slice: x: 2, y: 2, z: 4, core: 2. Of those that a mesh axis runs over, the one named last changes fastest.
Arguments:
- tokens: bfloat16 [4096, 2048], P(('dp', 'expert')), may hold values from -6 to 6
- out_grad: bfloat16 [4096, 2048], P(('dp', 'expert')), may hold values from -3 to 3
- z_weight: float32 [4096], P(('dp', 'expert')), may hold values from 0.1 to 1
- router_weight: bfloat16 [2048, 128], replicated, may hold values from -0.125 to 0.125
- expert_ids: int32 [4096, 4], P(('dp', 'expert')), may hold values from 0 to 127, as said below
- gate_up_weight: bfloat16 [4, 2048, 3072], P('expert'), may hold values from -0.125 to 0.125
- down_weight: bfloat16 [4, 1536, 2048], P('expert'), may hold values from -0.15625 to 0.15625
Outputs:
- token_grad: bfloat16 [4096, 2048], P(('dp', 'expert'))
- router_grad: float32 [2048, 128], replicated
- gate_up_grad: bfloat16 [4, 2048, 3072], P('expert', 'dp')
- down_grad: bfloat16 [4, 1536, 2048], P('expert', 'dp')
Inputs may be any that keep to these rules, and one draw needn't show every extreme that they name: `expert_ids`: each row names 4 different experts. Experts 0 to 3 are the ones in flight. The 128 rows of one device name any one expert in flight at most 64 times; in every data group some expert in flight is named exactly 64 times by the rows of each device of the group.
All inputs are finite; a program needn't handle non-finite values.
Results may differ from a plain program's by a relative error of at most 0.019.
Values may be sent and summed in bfloat16 or wider, within the bound.
A program may use at most 192 MiB of HBM per device.

v0:
```python
import jax
import jax.numpy as jnp
from jax import lax
from jax.sharding import PartitionSpec as P


def expert_rows(rows_in, rows_grad, w_gateup, w_down, acc_gateup, acc_down):
    hidden_units = w_down.shape[0]
    pre_act = jnp.dot(rows_in, w_gateup, preferred_element_type=jnp.float32)
    gate_pre = pre_act[:, :hidden_units]
    up_pre = pre_act[:, hidden_units:]
    activated = jax.nn.silu(gate_pre)
    hidden = (activated * up_pre).astype(jnp.bfloat16)
    expert_out = jnp.dot(hidden, w_down, preferred_element_type=jnp.float32).astype(jnp.bfloat16)
    hidden_grad = lax.dot_general(
        rows_grad, w_down, (((1,), (1,)), ((), ())), preferred_element_type=jnp.float32
    )
    acc_down = lax.dot_general(
        hidden, rows_grad, (((0,), (0,)), ((), ())), preferred_element_type=jnp.float32
    )
    sigmoid_gate = jax.nn.sigmoid(gate_pre)
    gate_grad = hidden_grad * up_pre * sigmoid_gate * (1.0 + gate_pre * (1.0 - sigmoid_gate))
    up_grad = hidden_grad * activated
    pre_grad = jnp.concatenate([gate_grad, up_grad], axis=1).astype(jnp.bfloat16)
    acc_gateup = lax.dot_general(
        rows_in, pre_grad, (((0,), (0,)), ((), ())), preferred_element_type=jnp.float32
    )
    input_grad = lax.dot_general(
        pre_grad, w_gateup, (((1,), (1,)), ((), ())), preferred_element_type=jnp.float32
    ).astype(jnp.bfloat16)
    return (acc_gateup, acc_down, expert_out, input_grad)


def split_pair(values):
    upper = values.astype(jnp.bfloat16)
    lower = (values - upper.astype(jnp.float32)).astype(jnp.bfloat16)
    return jnp.stack([upper, lower], axis=-1)


def join_pair(pair):
    return pair[..., 0].astype(jnp.float32) + pair[..., 1].astype(jnp.float32)


def per_device(tokens, out_grad, z_weight, router_weight, expert_ids, gate_up_weight, down_weight):
    tok_count, width = tokens.shape
    top_count = expert_ids.shape[1]
    routed = router_weight.shape[1]
    flight = lax.axis_size("expert")
    capacity = tok_count // 2
    w_gateup = gate_up_weight[0]
    w_down = down_weight[0]
    hidden_units = w_down.shape[0]
    logits = jnp.dot(tokens, router_weight, preferred_element_type=jnp.float32)
    choose = expert_ids[:, :, None] == jnp.arange(routed, dtype=jnp.int32)[None, None, :]
    selected = jnp.sum(jnp.where(choose, logits[:, None, :], 0.0), axis=2)
    sel_exp = jnp.exp(selected)
    probs = sel_exp / jnp.sum(sel_exp, axis=1, keepdims=True)
    log_total = jnp.log(jnp.sum(jnp.exp(logits), axis=1))
    flat_ids = expert_ids.reshape(-1)
    slot_count = tok_count * top_count
    member = (flat_ids[:, None] == jnp.arange(flight, dtype=jnp.int32)[None, :]).astype(jnp.int32)
    ranks = jnp.sum((jnp.cumsum(member, axis=0) - 1) * member, axis=1)
    in_flight = flat_ids < flight
    position = jnp.where(in_flight, flat_ids * capacity + ranks, flight * capacity)
    source_slot = (
        jnp.zeros((flight * capacity,), jnp.int32)
        .at[position]
        .set(jnp.arange(slot_count, dtype=jnp.int32), mode="drop")
    )
    filled = jnp.zeros((flight * capacity,), jnp.bool_).at[position].set(True, mode="drop")
    source_tok = source_slot // top_count
    send_in = jnp.where(filled[:, None], tokens[source_tok], 0)
    slot_prob = jnp.where(filled, probs.reshape(-1)[source_slot], 0.0)
    counts = jnp.sum(member, axis=0)
    count_msg = jnp.stack([counts // 128, counts % 128], axis=1).astype(jnp.bfloat16)
    send_raw = jnp.where(filled[:, None], out_grad[source_tok], 0)
    prob_pair = split_pair(slot_prob)
    recv_in, recv_raw, recv_prob, recv_counts = (
        lax.all_to_all(
            send_in.reshape(flight, capacity, width),
            "expert",
            split_axis=0,
            concat_axis=0,
            tiled=True,
        ),
        lax.all_to_all(
            send_raw.reshape(flight, capacity, width),
            "expert",
            split_axis=0,
            concat_axis=0,
            tiled=True,
        ),
        lax.all_to_all(
            prob_pair.reshape(flight, capacity, 2),
            "expert",
            split_axis=0,
            concat_axis=0,
            tiled=True,
        ),
        lax.all_to_all(count_msg, "expert", split_axis=0, concat_axis=0, tiled=True),
    )
    sources = recv_in.shape[0]
    total_rows = sources * capacity
    flat_in = recv_in.reshape(total_rows, width)
    flat_raw = recv_raw.reshape(total_rows, width)
    row_prob = join_pair(recv_prob.reshape(total_rows, 2))
    flat_grad = (row_prob[:, None] * flat_raw.astype(jnp.float32)).astype(jnp.bfloat16)
    acc_gateup, acc_down, produced, back_rows = expert_rows(
        flat_in,
        flat_grad,
        w_gateup,
        w_down,
        jnp.zeros((width, 2 * hidden_units), jnp.float32),
        jnp.zeros((hidden_units, width), jnp.float32),
    )
    slot_at = jnp.where(in_flight, position, 0)
    row_score = jnp.sum(flat_raw.astype(jnp.float32) * produced.astype(jnp.float32), axis=1)
    score_pair = split_pair(row_score)
    home_dx, home_pair = (
        lax.all_to_all(
            back_rows.reshape(sources, capacity, width),
            "expert",
            split_axis=0,
            concat_axis=0,
            tiled=True,
        ),
        lax.all_to_all(
            score_pair.reshape(sources, capacity, 2),
            "expert",
            split_axis=0,
            concat_axis=0,
            tiled=True,
        ),
    )
    flat_dx = home_dx.reshape(flight * capacity, width)
    flat_score = join_pair(home_pair.reshape(flight * capacity, 2))
    scores = jnp.where(in_flight, flat_score[slot_at], 0.0).reshape(tok_count, top_count)
    slot_dx = jnp.where(in_flight[:, None], flat_dx[slot_at], 0).reshape(
        tok_count, top_count, width
    )
    mean_score = jnp.sum(probs * scores, axis=1, keepdims=True)
    sel_grad = probs * (scores - mean_score)
    z_grad = 2.0 * z_weight[:, None] * log_total[:, None] * jnp.exp(logits - log_total[:, None])
    logit_grad = (z_grad + jnp.sum(jnp.where(choose, sel_grad[:, :, None], 0.0), axis=1)).astype(
        jnp.bfloat16
    )
    token_grad = (
        jnp.sum(slot_dx.astype(jnp.float32), axis=1)
        + lax.dot_general(
            logit_grad, router_weight, (((1,), (1,)), ((), ())), preferred_element_type=jnp.float32
        )
    ).astype(jnp.bfloat16)
    router_part = lax.dot_general(
        tokens, logit_grad, (((0,), (0,)), ((), ())), preferred_element_type=jnp.float32
    )
    router_grad = lax.psum(router_part, ("dp", "expert"))
    part_gateup = acc_gateup.astype(jnp.bfloat16)
    part_down = acc_down.astype(jnp.bfloat16)
    gate_up_grad, down_grad = (
        lax.psum_scatter(part_gateup[None], "dp", scatter_dimension=1, tiled=True).astype(
            jnp.float32
        ),
        lax.psum_scatter(part_down[None], "dp", scatter_dimension=1, tiled=True).astype(
            jnp.float32
        ),
    )
    return (
        token_grad,
        router_grad,
        gate_up_grad.astype(jnp.bfloat16),
        down_grad.astype(jnp.bfloat16),
    )


def solution(mesh):
    return jax.shard_map(
        per_device,
        mesh=mesh,
        in_specs=(
            P(("dp", "expert"), None),
            P(("dp", "expert"), None),
            P(("dp", "expert")),
            P(),
            P(("dp", "expert"), None),
            P("expert", None, None),
            P("expert", None, None),
        ),
        out_specs=(
            P(("dp", "expert"), None),
            P(),
            P("expert", "dp", None),
            P("expert", "dp", None),
        ),
        check_vma=False,
    )
```

profile of v0, /device:TPU:0, one launch (start us, length us, event | category | flops | bytes accessed | tf_op | source)
XLA Modules:
  0.0 440.1 jit_solution(1820209398362379599)
XLA Ops:
  8.0 0.7 broadcast_compare_fusion
  8.8 0.7 broadcast_multiply_fusion
  9.4 0.8 copy.45
  10.3 0.1 eq.38
  10.4 0.1 copy.42
  10.6 0.6 copy-done.5
  11.2 0.1 lt.55
  11.3 0.1 copy.44
  11.4 0.1 mul.92
  11.5 1.2 reduce-window.6
  12.8 0.2 slice_reduce_fusion
  13.0 0.2 reduce-window.9
  13.3 2.4 scatter_custom_fusion.1
  15.8 2.4 scatter_custom_fusion
  18.3 0.6 pad_clamp_fusion.1
  18.9 1.4 gather_fusion.2
  20.3 1.4 gather_fusion.1
  21.7 1.5 broadcast_select_fusion
  23.2 4.4 all-to-all-start.2
  27.6 0.4 exponential_reduce_fusion
  28.1 0.2 select_reduce_fusion.1
  28.3 0.6 multiply_multiply_fusion
  29.0 13.1 %all-to-all-done.2 = bf16[4,64,2048]{2,1,0:T(8,128)(2,1)S(1)} async-done(((bf16[4,64,2048]{2,1,0:T(8,128)(2,1)}), bf16[4,64,2048]{2,1,0:T(8,128)(2,1)S(1)}, u32[]{:S(2)}, u32[]{:S(2)}) %all-to-all-start.2) | async-done | bytes 1048608 | tf_op jit(solution)/shard_map/all_to_all | solution.py:79
  42.0 3.5 all-to-all-start.1
  45.6 9.7 %fusion.2 = f32[256,3072]{1,0:T(8,128)} fusion(bf16[256,2048]{1,0:T(8,128)(2,1)S(1)} %bitcast.81, bf16[1,2048,3072]{2,1,0:T(8,128)(2,1)} %param.12), kind=kOutput, calls=%fused_computation.9 | convolution fusion | flops 3221225472 | bytes 16777216 | tf_op jit(solution)/shard_map/dot_general | solution.py:9
  55.2 2.3 multiply_convert_fusion.1
  57.6 2.4 all-to-all-done.1
  60.0 4.8 %fusion.24 = f32[256]{0:T(256)S(1)} fusion(bf16[256,1536]{1,0:T(8,128)(2,1)S(1)} %multiply_convert_fusion.1, bf16[1,1536,2048]{2,1,0:T(8,128)(2,1)} %param.13, bf16[256,2048]{1,0:T(8,128)(2,1)S(1)} %bitcast.80), kind=kOutput, calls=%fused_computation.35 | convolution fusion | flops 1613233920 | bytes 8127488 | tf_op jit(solution)/shard_map/dot_general | solution.py:14
  64.8 0.6 copy.51
  65.4 3.4 all-to-all-start.4
  68.8 0.5 exponential_reduce_fusion.1
  69.4 3.0 all-to-all-done.4
  72.4 3.5 gather_fusion.4
  76.1 1.2 multiply_reduce_fusion
  77.3 0.6 copy-done.8
  77.9 0.1 copy.48
  78.0 0.1 div.31
  78.1 2.1 gather_fusion
  80.2 0.6 subtract_convert_fusion.1
  80.8 0.6 select_convert_fusion
  81.4 0.7 subtract_multiply_fusion
  82.2 0.6 copy.49
  82.8 3.2 all-to-all-start
  86.1 0.2 select_reduce_fusion
  86.3 0.7 copy.54
  87.0 0.9 add_convert_fusion
  87.9 1.3 convolution_bitcast_fusion
  89.2 0.5 all-to-all-done
  89.8 0.5 broadcast.186
  90.3 0.7 fusion.38
  91.0 0.2 fusion.22
  91.2 4.4 %fusion.4 = bf16[1,1536,2048]{2,1,0:T(8,128)(2,1)} fusion(bf16[256,1536]{1,0:T(8,128)(2,1)S(1)} %multiply_convert_fusion.1, bf16[256,2048]{1,0:T(8,128)(2,1)S(1)} %fusion.22), kind=kOutput, calls=%fused_computation.13 | convolution fusion | flops 1613758464 | bytes 8126464 | tf_op jit(solution)/shard_map/dot_general | solution.py:18
  95.8 0.2 multiply_convert_fusion
  96.1 6.0 %multiply_convert_fusion.3 = (bf16[256,1536]{1,0:T(8,128)(2,1)S(1)}, bf16[256,1536]{1,0:T(8,128)(2,1)S(1)}) fusion(f32[256,3072]{1,0:T(8,128)} %fusion.2, bf16[256,2048]{1,0:T(8,128)(2,1)S(1)} %bitcast.85, bf16[1,1536,2048]{2,1,0:T(8,128)(2,1)} %param.13), kind=kOutput, calls=%fused_computation.32 | convolution fusion | flops 1615724544 | bytes 12058624 | tf_op jit(solution)/shard_map/dot_general | solution.py:15
  102.1 6.6 %convert_bitcast_fusion = bf16[1,2048,3072]{2,1,0:T(8,128)(2,1)} fusion(bf16[256,2048]{1,0:T(8,128)(2,1)S(1)} %bitcast.82, bf16[256,1536]{1,0:T(8,128)(2,1)S(1)} %get-tuple-element.31, bf16[256,1536]{1,0:T(8,128)(2,1)S(1)} %get-tuple-element.30), kind=kOutput, calls=%fused_computation.11 | convolution fusion | flops 3230662656 | bytes 15204352 | tf_op jit(solution)/shard_map/dot_general | solution.py:25
  108.7 9.0 %fusion.18 = bf16[256,2048]{1,0:T(8,128)(2,1)} fusion(bf16[1,2048,3072]{2,1,0:T(8,128)(2,1)} %param.12, bf16[256,1536]{1,0:T(8,128)(2,1)S(1)} %get-tuple-element.31, bf16[256,1536]{1,0:T(8,128)(2,1)S(1)} %get-tuple-element.30), kind=kOutput, calls=%fused_computation.22 | convolution fusion | flops 3224895488 | bytes 15204352 | tf_op jit(solution)/shard_map/dot_general | solution.py:28
  117.8 3.9 all-to-all-start.3
  121.7 229.6 %all-reduce.2.cloned.1.call-done = f32[2048,128]{0,1:T(8,128)} async-done(((f32[2048,128]{0,1:T(8,128)}), f32[2048,128]{0,1:T(8,128)}) %all-reduce.2.cloned.1.call-update) | async-done | bytes 1048592 | tf_op jit(solution)/shard_map/psum | solution.py:156
  351.2 2.6 copy.55
  353.8 2.5 gather_fusion.3
  356.3 2.2 gather.29
  358.6 5.6 %convert_reduce_fusion = f32[128,2048]{1,0:T(8,128)S(1)} fusion(bf16[128,4,2048]{2,1,0:T(4,128)(2,1)} %gather.29, pred[128,4]{1,0:T(8,128)(4,1)S(1)} %copy-done.6), kind=kLoop, calls=%fused_computation.18 | loop fusion | flops 2883584 | bytes 3146240 | tf_op jit(solution)/shard_map/reduce_sum | solution.py:148
  364.1 1.1 fusion.21
  365.3 67.3 %reduce-scatter.3.cloned.1.call-done = bf16[1,256,3072]{2,1,0:T(8,128)(2,1)} async-done(((bf16[1,2048,3072]{2,1,0:T(8,128)(2,1)}), bf16[1,256,3072]{2,1,0:T(8,128)(2,1)}) %reduce-scatter.3.cloned.1.call-update) | async-done | bytes 1572880 | tf_op jit(solution)/shard_map/reduce_scatter | solution.py:160
  (57 shorter events, 1.4 us)
Async XLA Ops:
  8.0 10.9 %copy-start = (bf16[128,2048]{1,0:T(8,128)(2,1)S(1)}, bf16[128,2048]{1,0:T(8,128)(2,1)}, u32[]{:S(2)}) copy-start(bf16[128,2048]{1,0:T(8,128)(2,1)} %param.7) | copy-start | bytes 1572868
  10.6 0.6 copy-start.5
  18.2 0.7 copy-start.11
  18.9 1.4 copy-start.2
  23.2 4.4 %copy-start.3 = (bf16[2048,128]{1,0:T(8,128)(2,1)S(1)}, bf16[2048,128]{1,0:T(8,128)(2,1)}, u32[]{:S(2)}) copy-start(bf16[2048,128]{1,0:T(8,128)(2,1)} %param.10) | copy-start | bytes 1572868
  23.2 4.9 %copy-start.7 = (s32[128,4]{0,1:T(4,128)S(1)}, s32[128,4]{0,1:T(4,128)}, u32[]{:S(2)}) copy-start(s32[128,4]{0,1:T(4,128)} %param.11) | copy-start | bytes 6148
  23.2 5.1 %copy-start.12 = (f32[128]{0:T(128)S(1)}, f32[128]{0:T(128)}, u32[]{:S(2)}) copy-start(f32[128]{0:T(128)} %param.9) | copy-start | bytes 1540
  23.2 18.8 %all-to-all-start.2 = ((bf16[4,64,2048]{2,1,0:T(8,128)(2,1)}), bf16[4,64,2048]{2,1,0:T(8,128)(2,1)S(1)}, u32[]{:S(2)}, u32[]{:S(2)}) async-start(bf16[4,64,2048]{2,1,0:T(8,128)(2,1)} %get-tuple-element.38), calls=%async_computation.2 | async-start | bytes 2097152 | tf_op jit(solution)/shard_map/all_to_all | solution.py:79
  28.1 44.3 %copy-start.9 = (s32[1024]{0:T(1024)}, s32[1024]{0:T(1024)S(1)}, u32[]{:S(2)}) copy-start(s32[1024]{0:T(1024)S(1)} %pad_clamp_fusion) | copy-start | bytes 12292
  42.0 17.9 %all-to-all-start.1 = ((bf16[4,64,2048]{2,1,0:T(8,128)(2,1)}), bf16[4,64,2048]{2,1,0:T(8,128)(2,1)S(1)}, u32[]{:S(2)}, u32[]{:S(2)}) async-start(bf16[4,64,2048]{2,1,0:T(8,128)(2,1)} %get-tuple-element.39), calls=%async_computation.1 | async-start | bytes 2097152 | tf_op jit(solution)/shard_map/all_to_all | solution.py:86
  65.4 6.9 %all-to-all-start.4 = ((bf16[4,64,2]{1,2,0:T(2,128)(2,1)}), bf16[4,64,2]{1,2,0:T(2,128)(2,1)S(1)}, u32[]{:S(2)}, u32[]{:S(2)}) async-start(bf16[4,64,2]{1,2,0:T(2,128)(2,1)} %copy.51), calls=%async_computation.4 | async-start | bytes 4096 | tf_op jit(solution)/shard_map/all_to_all | solution.py:127
  77.3 0.6 copy-start.8
  82.8 6.9 %all-to-all-start = ((bf16[4,64,2]{1,2,0:T(2,128)(2,1)}), bf16[4,64,2]{1,2,0:T(2,128)(2,1)S(1)}, u32[]{:S(2)}, u32[]{:S(2)}) async-start(bf16[4,64,2]{1,2,0:T(2,128)(2,1)} %copy.49), calls=%async_computation | async-start | bytes 4096 | tf_op jit(solution)/shard_map/all_to_all | solution.py:93
  86.0 265.2 %all-reduce.2.cloned.1.call-start = ((), (), s32[]{:S(2)}) async-start(), calls=%async_computation.7 | async-start | bytes 2097152 | tf_op jit(solution)/shard_map/psum | solution.py:156
  89.2 276.1 %reduce-scatter.5.cloned.1.call-start = ((), (), s32[]{:S(2)}) async-start(), calls=%async_computation.9 | async-start | bytes 7077888 | tf_op jit(solution)/shard_map/reduce_scatter | solution.py:163
  95.7 336.9 %reduce-scatter.3.cloned.1.call-start = ((), (), s32[]{:S(2)}) async-start(), calls=%async_computation.8 | async-start | bytes 14155776 | tf_op jit(solution)/shard_map/reduce_scatter | solution.py:160
  117.8 236.0 %copy-start.10 = (s32[1024]{0:T(1024)S(1)}, s32[1024]{0:T(1024)}, u32[]{:S(2)}) copy-start(s32[1024]{0:T(1024)} %copy-done.9) | copy-start | bytes 12292
  117.8 236.0 %all-to-all-start.3 = ((bf16[4,64,2048]{2,1,0:T(8,128)(2,1)}), bf16[4,64,2048]{2,1,0:T(8,128)(2,1)S(1)}, u32[]{:S(2)}, u32[]{:S(2)}) async-start(bf16[4,64,2048]{2,1,0:T(8,128)(2,1)} %bitcast.9), calls=%async_computation.3 | async-start | bytes 2097152 | tf_op jit(solution)/shard_map/all_to_all | solution.py:120
  356.3 2.3 copy-start.6
  356.3 76.3 %copy-start.1 = (bf16[128,2048]{1,0:T(8,128)(2,1)S(1)}, bf16[128,2048]{1,0:T(8,128)(2,1)}, u32[]{:S(2)}) copy-start(bf16[128,2048]{1,0:T(8,128)(2,1)} %param.7) | copy-start | bytes 1572868
  358.6 5.6 %copy-start.4 = (bf16[2048,128]{1,0:T(8,128)(2,1)S(1)}, bf16[2048,128]{1,0:T(8,128)(2,1)}, u32[]{:S(2)}) copy-start(bf16[2048,128]{1,0:T(8,128)(2,1)} %param.10) | copy-start | bytes 1572868
Sparse Core Ops, SparseCore 0:
  92.6 258.5 all-reduce.1
Sparse Core Ops, SparseCore 1:
  95.8 123.6 reduce-scatter.4
  223.5 209.1 reduce-scatter.2
where the time goes:
time: 441 us; the launch traced here: 440 us
  waiting for transfers between devices  316 us (72%)
  matrix products  43.3 us (10%)
  local copies, waits for them, and re-layouts  26.9 us (6%)
  other arithmetic  19.7 us (4%)
  starting transfers between devices  18.5 us (4%)
  between operations  15.8 us (4%)
    psum x1, waiting for transfers between devices, per_device(): router_grad = lax.psum(router_part, ('dp', 'expert'))  230 us
    reduce_scatter x1, waiting for transfers between devices, per_device(): lax.psum_scatter(part_gateup[None], 'dp', scatter_dimension=1, tiled=True)  67.3 us
    all_to_all x1, waiting for transfers between devices, per_device(): lax.all_to_all(send_in.reshape(flight, capacity, width), 'expert', split_...  13.1 us
    dot_general x1, matrix products, expert_rows(): pre_act = jnp.dot(rows_in, w_gateup, preferred_element_type=jnp.float32)  9.69 us
    dot_general x1, matrix products, expert_rows(): lax.dot_general(pre_grad, w_gateup, (((1,), (1,)), ((), ())), preferred_e...  9.05 us
  transfers between devices with their start and end apart: 8, of which 6 were waited for; matrix products, arithmetic and copies ran while one was open for 13% of the time, Pallas kernels for 0%

commit v1 on v0

--- a/solution.py
+++ b/solution.py
@@ -153,7 +153,7 @@
     router_part = lax.dot_general(
         tokens, logit_grad, (((0,), (0,)), ((), ())), preferred_element_type=jnp.float32
     )
-    router_grad = lax.psum(router_part, ("dp", "expert"))
+    router_grad = jax.lax.psum(jax.lax.psum(router_part, axis_name="dp"), axis_name="expert")
     part_gateup = acc_gateup.astype(jnp.bfloat16)
     part_down = acc_down.astype(jnp.bfloat16)
     gate_up_grad, down_grad = (

time: 441 us -> 544 us (1.23)
  waiting for transfers between devices: 316 us -> 403 us
  blocking collectives: 0 us -> 29 us
  starting transfers between devices: 18.5 us -> 11.5 us
    psum x1 -> x2, waiting for transfers between devices: 230 us -> 69.5 us  [the longest x1 69.5 us: per_device(): jax.lax.psum(router_part, axis_name='dp')]
    reduce_scatter x1, waiting for transfers between devices: 67.3 us -> 211 us  [per_device(): lax.psum_scatter(part_gateup[None], 'dp', scatter_dimension=1, tiled=True)]
    reduce_scatter x1, waiting for transfers between devices: 0.01 us -> 105 us  [per_device(): lax.psum_scatter(part_down[None], 'dp', scatter_dimension=1, tiled=True)]
    all_to_all x0 -> x2, blocking collectives: none -> 29 us  [the longest x1 22.9 us: per_device(): lax.all_to_all(back_rows.reshape(sources, capacity, width), 'expert', spl...]
    all_to_all x2 -> x0, starting transfers between devices: 7.09 us -> none  [the longest x1 3.87 us: per_device(): lax.all_to_all(back_rows.reshape(sources, capacity, width), 'expert', spl...]
  transfers between devices with their start and end apart: 8 -> 7, of which waited for: 6 -> 6; matrix products, arithmetic and copies ran while one was open for 13% -> 11% of each run, Pallas kernels for 0% -> 0%
where the time goes in v1:
time: 544 us
  waiting for transfers between devices  403 us (74%)
  matrix products  42.6 us (8%)
  blocking collectives  29 us (5%)
  local copies, waits for them, and re-layouts  25.7 us (5%)
  other arithmetic  17.3 us (3%)
  between operations  14.1 us (3%)
  starting transfers between devices  11.5 us (2%)
    reduce_scatter x1, waiting for transfers between devices, per_device(): lax.psum_scatter(part_gateup[None], 'dp', scatter_dimension=1, tiled=True)  211 us
    reduce_scatter x1, waiting for transfers between devices, per_device(): lax.psum_scatter(part_down[None], 'dp', scatter_dimension=1, tiled=True)  105 us
    psum x1, waiting for transfers between devices, per_device(): jax.lax.psum(router_part, axis_name='dp')  69.5 us
    all_to_all x1, blocking collectives, per_device(): lax.all_to_all(back_rows.reshape(sources, capacity, width), 'expert', spl...  22.9 us
    all_to_all x1, waiting for transfers between devices, per_device(): lax.all_to_all(send_in.reshape(flight, capacity, width), 'expert', split_...  13.1 us
  transfers between devices with their start and end apart: 7, of which 6 were waited for; matrix products, arithmetic and copies ran while one was open for 11% of the time, Pallas kernels for 0%

profile of v1, /device:TPU:0, one launch (start us, length us, event | category | flops | bytes accessed | tf_op | source)
XLA Modules:
  0.0 543.6 jit_solution(13013839891197101313)
XLA Ops:
  7.2 0.7 broadcast_compare_fusion
  7.9 0.7 broadcast_multiply_fusion
  8.6 0.8 copy.45
  9.4 0.1 eq.42
  9.5 0.1 eq.38
  9.6 0.1 copy.42
  9.8 0.6 copy-done.5
  10.4 0.1 lt.55
  10.5 0.1 copy.44
  10.6 0.1 mul.92
  10.7 1.2 reduce-window.6
  11.9 0.2 slice_reduce_fusion
  12.1 0.2 reduce-window.9
  12.5 2.4 scatter_custom_fusion.1
  14.9 2.4 scatter_custom_fusion
  17.5 0.6 pad_clamp_fusion.1
  18.1 1.4 gather_fusion.2
  19.5 1.4 gather_fusion.1
  20.8 1.5 broadcast_select_fusion
  22.4 4.4 all-to-all-start.2
  26.8 0.4 exponential_reduce_fusion
  27.1 0.1 copy.47
  27.3 0.2 select_reduce_fusion.1
  27.5 0.5 multiply_multiply_fusion
  28.1 13.1 %all-to-all-done.2 = bf16[4,64,2048]{2,1,0:T(8,128)(2,1)S(1)} async-done(((bf16[4,64,2048]{2,1,0:T(8,128)(2,1)}), bf16[4,64,2048]{2,1,0:T(8,128)(2,1)S(1)}, u32[]{:S(2)}, u32[]{:S(2)}) %all-to-all-start.2) | async-done | bytes 1048608 | tf_op jit(solution)/shard_map/all_to_all | solution.py:79
  41.2 3.5 all-to-all-start.1
  44.7 9.7 %fusion.2 = f32[256,3072]{1,0:T(8,128)} fusion(bf16[256,2048]{1,0:T(8,128)(2,1)S(1)} %bitcast.81, bf16[1,2048,3072]{2,1,0:T(8,128)(2,1)} %param.12), kind=kOutput, calls=%fused_computation.9 | convolution fusion | flops 3221225472 | bytes 16777216 | tf_op jit(solution)/shard_map/dot_general | solution.py:9
  54.4 2.3 multiply_convert_fusion.1
  56.7 2.4 all-to-all-done.1
  59.1 4.8 fusion.24
  64.0 0.6 copy.51
  64.6 3.2 all-to-all-start.4
  67.8 0.2 all-reduce.3.cloned.1.call-start
  68.0 0.5 exponential_reduce_fusion.1
  68.6 2.9 all-to-all-done.4
  71.5 0.1 reshape.205
  71.6 3.5 gather_fusion.4
  75.1 0.1 gather.31
  75.3 0.7 multiply_reduce_fusion
  76.0 0.2 select_reduce_fusion
  76.2 0.7 copy.54
  76.9 0.9 add_convert_fusion
  77.8 1.3 convolution_bitcast_fusion
  79.1 0.1 copy.48
  79.2 0.1 div.31
  79.3 2.1 gather_fusion
  81.7 6.1 %all_to_all.25 = bf16[4,64,2]{1,2,0:T(2,128)(2,1)S(1)} all-to-all(bf16[4,64,2]{1,2,0:T(2,128)(2,1)S(1)} %copy.49), channel_id=1, replica_groups=mesh['dp'=8,'expert'=4] {'expert'}, dimensions={0} | all-to-all | bytes 2048 | tf_op jit(solution)/shard_map/all_to_all | solution.py:93
  87.9 0.5 broadcast.186
  88.4 0.7 fusion.38
  89.0 69.5 %all-reduce.3.cloned.1.call-done = f32[2048,128]{0,1:T(8,128)} async-done(((f32[2048,128]{0,1:T(8,128)}), f32[2048,128]{0,1:T(8,128)}) %all-reduce.3.cloned.1.call-update) | async-done | bytes 1048592 | tf_op jit(solution)/shard_map/psum | solution.py:156
  158.6 0.2 fusion.22
  158.8 4.4 fusion.4
  163.4 0.2 multiply_convert_fusion
  163.7 6.2 %multiply_convert_fusion.3 = (bf16[256,1536]{1,0:T(8,128)(2,1)S(1)}, bf16[256,1536]{1,0:T(8,128)(2,1)S(1)}) fusion(f32[256,3072]{1,0:T(8,128)} %fusion.2, bf16[256,2048]{1,0:T(8,128)(2,1)S(1)} %bitcast.85, bf16[1,1536,2048]{2,1,0:T(8,128)(2,1)} %param.13), kind=kOutput, calls=%fused_computation.32 | convolution fusion | flops 1615724544 | bytes 12058624 | tf_op jit(solution)/shard_map/dot_general | solution.py:15
  169.9 6.6 %convert_bitcast_fusion = bf16[1,2048,3072]{2,1,0:T(8,128)(2,1)} fusion(bf16[256,2048]{1,0:T(8,128)(2,1)S(1)} %bitcast.82, bf16[256,1536]{1,0:T(8,128)(2,1)S(1)} %get-tuple-element.31, bf16[256,1536]{1,0:T(8,128)(2,1)S(1)} %get-tuple-element.30), kind=kOutput, calls=%fused_computation.11 | convolution fusion | flops 3230662656 | bytes 15204352 | tf_op jit(solution)/shard_map/dot_general | solution.py:25
  176.5 8.1 %fusion.18 = bf16[256,2048]{1,0:T(8,128)(2,1)S(1)} fusion(bf16[1,2048,3072]{2,1,0:T(8,128)(2,1)} %param.12, bf16[256,1536]{1,0:T(8,128)(2,1)S(1)} %get-tuple-element.31, bf16[256,1536]{1,0:T(8,128)(2,1)S(1)} %get-tuple-element.30), kind=kOutput, calls=%fused_computation.22 | convolution fusion | flops 3224895488 | bytes 15204352 | tf_op jit(solution)/shard_map/dot_general | solution.py:28
  184.7 22.9 %all_to_all.26 = bf16[4,64,2048]{2,1,0:T(8,128)(2,1)S(1)} all-to-all(bf16[4,64,2048]{2,1,0:T(8,128)(2,1)S(1)} %bitcast.86), channel_id=1, replica_groups=mesh['dp'=8,'expert'=4] {'expert'}, dimensions={0} | all-to-all | bytes 2097152 | tf_op jit(solution)/shard_map/all_to_all | solution.py:120
  207.6 2.5 gather_fusion.3
  210.1 2.2 gather.29
  212.3 5.6 %convert_reduce_fusion = f32[128,2048]{1,0:T(8,128)S(1)} fusion(bf16[128,4,2048]{2,1,0:T(4,128)(2,1)} %gather.29, pred[128,4]{1,0:T(8,128)(4,1)S(1)} %copy-done.6), kind=kLoop, calls=%fused_computation.18 | loop fusion | flops 2883584 | bytes 3146240 | tf_op jit(solution)/shard_map/reduce_sum | solution.py:148
  217.9 1.1 fusion.21
  219.1 2.5 copy.55
  221.6 104.8 %reduce-scatter.5.cloned.1.call-done = bf16[1,192,2048]{2,1,0:T(8,128)(2,1)} async-done(((bf16[1,1536,2048]{2,1,0:T(8,128)(2,1)}), bf16[1,192,2048]{2,1,0:T(8,128)(2,1)}) %reduce-scatter.5.cloned.1.call-update) | async-done | bytes 786448 | tf_op jit(solution)/shard_map/reduce_scatter | solution.py:163
  326.4 210.7 %reduce-scatter.3.cloned.1.call-done = bf16[1,256,3072]{2,1,0:T(8,128)(2,1)} async-done(((bf16[1,2048,3072]{2,1,0:T(8,128)(2,1)}), bf16[1,256,3072]{2,1,0:T(8,128)(2,1)}) %reduce-scatter.3.cloned.1.call-update) | async-done | bytes 1572880 | tf_op jit(solution)/shard_map/reduce_scatter | solution.py:160
  (58 shorter events, 1.0 us)
Async XLA Ops:
  7.2 10.9 %copy-start = (bf16[128,2048]{1,0:T(8,128)(2,1)S(1)}, bf16[128,2048]{1,0:T(8,128)(2,1)}, u32[]{:S(2)}) copy-start(bf16[128,2048]{1,0:T(8,128)(2,1)} %param.7) | copy-start | bytes 1572868
  9.8 0.6 copy-start.5
  17.4 0.7 copy-start.10
  18.1 1.4 copy-start.2
  22.4 4.4 copy-start.3
  22.4 4.9 copy-start.7
  22.4 5.1 copy-start.12
  22.4 18.8 %all-to-all-start.2 = ((bf16[4,64,2048]{2,1,0:T(8,128)(2,1)}), bf16[4,64,2048]{2,1,0:T(8,128)(2,1)S(1)}, u32[]{:S(2)}, u32[]{:S(2)}) async-start(bf16[4,64,2048]{2,1,0:T(8,128)(2,1)} %get-tuple-element.38), calls=%async_computation.2 | async-start | bytes 2097152 | tf_op jit(solution)/shard_map/all_to_all | solution.py:79
  27.2 44.3 %copy-start.8 = (s32[1024]{0:T(1024)}, s32[1024]{0:T(1024)S(1)}, u32[]{:S(2)}) copy-start(s32[1024]{0:T(1024)S(1)} %pad_clamp_fusion) | copy-start | bytes 12292
  41.2 17.9 %all-to-all-start.1 = ((bf16[4,64,2048]{2,1,0:T(8,128)(2,1)}), bf16[4,64,2048]{2,1,0:T(8,128)(2,1)S(1)}, u32[]{:S(2)}, u32[]{:S(2)}) async-start(bf16[4,64,2048]{2,1,0:T(8,128)(2,1)} %get-tuple-element.39), calls=%async_computation.1 | async-start | bytes 2097152 | tf_op jit(solution)/shard_map/all_to_all | solution.py:86
  64.6 6.9 %all-to-all-start.4 = ((bf16[4,64,2]{1,2,0:T(2,128)(2,1)}), bf16[4,64,2]{1,2,0:T(2,128)(2,1)S(1)}, u32[]{:S(2)}, u32[]{:S(2)}) async-start(bf16[4,64,2]{1,2,0:T(2,128)(2,1)} %copy.51), calls=%async_computation.4 | async-start | bytes 4096 | tf_op jit(solution)/shard_map/all_to_all | solution.py:127
  67.8 90.7 %all-reduce.3.cloned.1.call-start = ((), (), s32[]{:S(2)}) async-start(), calls=%async_computation.7 | async-start | bytes 2097152 | tf_op jit(solution)/shard_map/psum | solution.py:156
  76.0 5.5 %copy-start.11 = (pred[256]{0:T(512)(128)(4,1)S(1)}, pred[256]{0:T(512)(128)(4,1)}, u32[]{:S(2)}) copy-start(pred[256]{0:T(512)(128)(4,1)} %copy-done.10) | copy-start | bytes 772
  79.1 140.0 %all-reduce.5.cloned.1.call-start = ((), (), s32[]{:S(2)}) async-start(), calls=%async_computation.8 | async-start | bytes 2097152 | tf_op jit(solution)/shard_map/psum | solution.py:156
  158.5 167.8 %reduce-scatter.5.cloned.1.call-start = ((), (), s32[]{:S(2)}) async-start(), calls=%async_computation.10 | async-start | bytes 7077888 | tf_op jit(solution)/shard_map/reduce_scatter | solution.py:163
  163.3 373.8 %reduce-scatter.3.cloned.1.call-start = ((), (), s32[]{:S(2)}) async-start(), calls=%async_computation.9 | async-start | bytes 14155776 | tf_op jit(solution)/shard_map/reduce_scatter | solution.py:160
  184.7 22.9 %copy-start.9 = (s32[1024]{0:T(1024)S(1)}, s32[1024]{0:T(1024)}, u32[]{:S(2)}) copy-start(s32[1024]{0:T(1024)} %copy-done.8) | copy-start | bytes 12292
  210.1 2.3 copy-start.6
  212.3 5.6 %copy-start.4 = (bf16[2048,128]{1,0:T(8,128)(2,1)S(1)}, bf16[2048,128]{1,0:T(8,128)(2,1)}, u32[]{:S(2)}) copy-start(bf16[2048,128]{1,0:T(8,128)(2,1)} %param.10) | copy-start | bytes 1572868
  212.3 324.8 %copy-start.1 = (bf16[128,2048]{1,0:T(8,128)(2,1)S(1)}, bf16[128,2048]{1,0:T(8,128)(2,1)}, u32[]{:S(2)}) copy-start(bf16[128,2048]{1,0:T(8,128)(2,1)} %param.7) | copy-start | bytes 1572868
Sparse Core Ops, SparseCore 0:
  79.2 79.2 all-reduce.2
  160.9 42.0 all-reduce.4
  207.1 119.2 reduce-scatter.4
  330.4 206.6 reduce-scatter.2
